TPU v7x, 512 devices: a whole 4x8x8 slice. The times are simulated.
512 devices in a mesh: dp: 64 (over z_hi, x, y), expert: 8 (over z_lo, core).
Axes of the slice: x: 4, y: 8, z: 8 (z_hi: 2, z_lo: 4; z = z_hi * 4 + z_lo), core: 2. Of those that a mesh axis runs over, the one named last changes fastest.
Arguments:
- tokens: bfloat16 [65536, 3072], P('dp'), may hold values from -16 to 16
- hidden_grads: bfloat16 [65536, 1024], P('dp', 'expert'), may hold values from -6 to 6
- routed: int32 [64], P('dp'), may hold values from 1 to 1024, 49152 in all
- master: float32 [2, 8192, 3072], P(None, 'expert', 'dp'), may hold values from -6 to 6
- moment_one: float32 [2, 1024, 3072], P(None, 'expert', 'dp'), may hold values from -3 to 3
- moment_two: float32 [2, 1024, 3072], P(None, 'expert', 'dp'), may hold values from 0.05 to 1
- hot_units: int32 [1024], P('expert'), may hold values from 0 to 1023, as said below
- cold_blocks: float32 [2, 8192, 3072], P(None, 'expert', 'dp'), may hold values from -6 to 6
- cold_shift: int32 [8192], P('expert'), may hold values from 0 to 7, as said below
Outputs:
- new_master: float32 [2, 8192, 3072], P(None, 'expert', 'dp')
- new_moment_one: float32 [2, 1024, 3072], P(None, 'expert', 'dp')
- new_moment_two: float32 [2, 1024, 3072], P(None, 'expert', 'dp')
Inputs may be any that keep to these rules, and one draw needn't show every extreme that they name: `routed`: the counts sum to 49152 and one of them equals 1024. `hot_units`: within each aligned block of 128 entries the values are distinct. `cold_shift`: within each aligned block of 1024 entries every value occurs exactly 8192 // 8 // 8 times.
All inputs are finite; a program needn't handle non-finite values. No bound on the sum of `routed` on one device may be relied on, other than what follows from the above.
Results may differ from a plain program's by a relative error of at most 0.003.
Values may be sent and summed in bfloat16 or wider, within the bound.
A program may use at most 64 MiB of HBM per device.

v0:
```python
import jax
import jax.numpy as jnp
from jax import lax
from jax.sharding import Mesh
from jax.sharding import PartitionSpec as P

D = 3072
DP = ("dp_0", "dp_1", "dp_2")
beta_one = 0.9
beta_two = 0.95
step_rate = 0.1
adam_eps = 1e-08


def joined_along(tiles, dim):
    tiles = jnp.moveaxis(tiles, 0, dim)
    shape = tiles.shape
    return tiles.reshape(*shape[:dim], shape[dim] * shape[dim + 1], *shape[dim + 2 :])


def sent_to_all(value, axis):
    copies = jnp.broadcast_to(value, (lax.axis_size(axis), *value.shape))
    return lax.all_to_all(copies, axis, split_axis=0, concat_axis=0, tiled=True)


def collect(value, axis, dim):
    return joined_along(sent_to_all(value, axis), dim)


def stacked_from(value, axes, order):
    tiles = value[None]
    for k in order:
        tiles = lax.all_gather(tiles, axes[k], axis=0, tiled=True)
    block = [lax.axis_size(axes[k]) for k in reversed(order)]
    tiles = tiles.reshape(*block, *value.shape)
    turned = sorted(range(len(order)), key=lambda place: order[len(order) - 1 - place])
    return tiles.transpose(*turned, *range(len(order), tiles.ndim)).reshape(-1, *value.shape)


def gather_axes(value, axes, order, dim):
    return joined_along(stacked_from(value, axes, order), dim)


def cut_along(value, dim, peers):
    before, after = (value.shape[:dim], value.shape[dim + 1 :])
    return jnp.moveaxis(value.reshape(*before, peers, -1, *after), dim, 0)


def sum_at_owner(value, axis, dim):
    tiles = cut_along(value, dim, lax.axis_size(axis))
    arrived = lax.all_to_all(tiles, axis, split_axis=0, concat_axis=0, tiled=True)
    return arrived.sum(axis=0)


def sum_in_two_steps(value, axes, dim):
    far, near = axes
    own = sum_at_owner(cut_along(value, dim, lax.axis_size(far)), near, dim + 1)
    return jnp.sum(lax.all_to_all(own, far, 0, 0, tiled=True), axis=0)


def contract_last(left, right):
    return lax.dot_general(
        left, right, (((1,), (1,)), ((), ())), preferred_element_type=jnp.float32
    )


def contract_first(left, right):
    return lax.dot_general(
        left, right, (((0,), (0,)), ((), ())), preferred_element_type=jnp.float32
    )


def rows_with(shift_row, wanted, capacity):
    span = shift_row.shape[0]
    places = jnp.arange(span, dtype=jnp.int32)
    sort_key = jnp.where(shift_row == wanted, places, places + span)
    return jnp.argsort(sort_key, stable=True)[:capacity]


def return_cold(cold_blocks, cold_shift):
    cycle_size = lax.axis_size("expert")
    span = cold_shift.shape[0]
    capacity = span // cycle_size
    cycle_index = lax.axis_index("expert")
    owner_shift = collect(cold_shift, "expert", 0).reshape(cycle_size, span)
    places = jnp.arange(cycle_size, dtype=jnp.int32)
    send_rows = jax.vmap(lambda row, wanted: rows_with(row, wanted, capacity))(
        owner_shift, (places - cycle_index) % cycle_size
    )
    packed = cold_blocks[:, send_rows.reshape(-1), :].reshape(
        2, cycle_size, capacity, cold_blocks.shape[2]
    )
    arrived = lax.all_to_all(packed, "expert", split_axis=1, concat_axis=1, tiled=True)
    take_rows = jax.vmap(lambda wanted: rows_with(cold_shift, wanted, capacity))(
        (cycle_index - places) % cycle_size
    )
    received = (
        jnp.zeros_like(cold_blocks)
        .at[:, take_rows.reshape(-1), :]
        .set(arrived.reshape(2, cycle_size * capacity, cold_blocks.shape[2]))
    )
    return received


def per_device(
    tokens, hidden_grads, routed, master, moment_one, moment_two, hot_units, cold_blocks, cold_shift
):
    weight_scale = D ** (-0.5)
    tok_count = tokens.shape[0]
    master_hot = master[:, hot_units, :]
    weights = master_hot.astype(jnp.bfloat16)
    weight_piece = gather_axes(weights, DP, (0, 1, 2), 2)
    gate_sum = contract_last(tokens, weight_piece[0])
    up_sum = contract_last(tokens, weight_piece[1])
    gate_pre = gate_sum * weight_scale
    up_pre = up_sum * weight_scale
    live_rows = (jnp.arange(tok_count, dtype=jnp.int32) < routed[0]).astype(jnp.float32)[:, None]
    cotangent = hidden_grads.astype(jnp.float32)
    sigmoid = jax.nn.sigmoid(gate_pre)
    d_up = (live_rows * cotangent * gate_pre * sigmoid).astype(jnp.bfloat16)
    d_gate = (live_rows * cotangent * up_pre * sigmoid * (1.0 + gate_pre * (1.0 - sigmoid))).astype(
        jnp.bfloat16
    )
    partial_value = (
        jnp.stack([contract_first(d_gate, tokens), contract_first(d_up, tokens)]) * weight_scale
    )
    grad_shard = sum_in_two_steps(partial_value, ("dp_0", ("dp_1", "dp_2")), 2)
    first_new = beta_one * moment_one + (1.0 - beta_one) * grad_shard
    second_new = beta_two * moment_two + (1.0 - beta_two) * grad_shard * grad_shard
    adam = master_hot - step_rate * first_new / (jnp.sqrt(second_new) + adam_eps)
    received = return_cold(cold_blocks, cold_shift)
    new_master = received.at[:, hot_units, :].set(adam)
    return (new_master, first_new, second_new)


def solution(mesh):
    finer = Mesh(
        mesh.devices.reshape(2, 4, 8, mesh.shape["expert"]), ("dp_0", "dp_1", "dp_2", "expert")
    )
    placed = (
        P(DP, None),
        P(DP, "expert"),
        P(DP),
        P(None, "expert", DP),
        P(None, "expert", DP),
        P(None, "expert", DP),
        P("expert"),
        P(None, "expert", DP),
        P("expert"),
    )
    return jax.shard_map(
        per_device,
        mesh=finer,
        in_specs=placed,
        out_specs=(P(None, "expert", DP), P(None, "expert", DP), P(None, "expert", DP)),
        check_vma=False,
    )
```

profile of v0, /device:TPU:1, one launch (start us, length us, event | category | flops | bytes accessed | tf_op | source)
XLA Modules:
  0.0 243.7 jit_solution(8984062820681312506)
XLA Ops:
  8.0 0.0 all-gather.3.cloned.1.call-start
  8.0 0.7 compare_select_fusion.2
  8.7 1.4 copy.106
  10.1 0.7 gather_fusion.1
  10.9 0.1 copy.107
  11.0 0.0 copy-start.1
  11.0 11.4 %all-gather = bf16[4,128,48]{1,2,0:T(8,128)(2,1)S(1)} all-gather(bf16[2,128,48]{1,2,0:T(8,128)(2,1)S(1)} %bitcast_convert_fusion), channel_id=2, replica_groups=mesh['dp_0'=2,'dp_1'=4,'dp_2'=8,'expert'=8] {'dp_0'}, dimensions={0}, use_global_device_ids=true | all-gather | bytes 73728 | tf_op jit(solution)/shard_map/all_gather | solution.py:33
  22.4 10.7 %all_gather.10 = bf16[8,2,128,48]{2,3,1,0:T(8,128)(2,1)} all-gather(bf16[2,2,128,48]{2,3,1,0:T(8,128)(2,1)S(1)} %bitcast.71), channel_id=1, replica_groups=mesh['dp_0'=2,'dp_1'=4,'dp_2'=8,'expert'=8] {'dp_1'}, dimensions={0}, use_global_device_ids=true | all-gather | bytes 245760 | tf_op jit(solution)/shard_map/all_gather | solution.py:33
  33.2 0.0 all-gather.3.cloned.1.call-update
  33.2 1.3 broadcast_in_dim.42
  34.5 9.8 %all-to-all-start = ((s32[8,1,1024]{2,1,0:T(1,128)}), s32[8,1,1024]{2,1,0:T(1,128)}, u32[]{:S(2)}, u32[]{:S(2)}) async-start(s32[8,1,1024]{2,1,0:T(1,128)} %broadcast_in_dim.42), calls=%async_computation | async-start | bytes 65536 | tf_op jit(solution)/shard_map/all_to_all | solution.py:23
  44.3 1.1 copy.108
  46.0 29.6 %all-gather.3.cloned.1.call-done = bf16[64,2,128,48]{2,3,1,0:T(8,128)(2,1)} async-done(((bf16[8,2,128,48]{2,3,1,0:T(8,128)(2,1)}), bf16[64,2,128,48]{2,3,1,0:T(8,128)(2,1)}) %all-gather.3.cloned.1.call-update) | async-done | bytes 1572880 | tf_op jit(solution)/shard_map/all_gather | solution.py:33
  75.6 0.0 copy-done.1
  75.6 0.0 copy-start
  75.6 1.7 copy.109
  77.3 0.1 fusion.25
  77.5 1.4 copy-done
  78.9 2.2 fusion
  81.1 3.8 %fusion.10 = f32[128,3072]{0,1:T(8,128)} fusion(bf16[1024,3072]{1,0:T(8,128)(2,1)S(1)} %copy-done, f32[1024,128]{0,1:T(8,128)S(1)} %fusion, bf16[1024,128]{0,1:T(8,128)(2,1)S(1)} %copy.108, f32[1024]{0:T(1024)S(1)} %fusion.18), kind=kOutput, calls=%fused_computation.21 | convolution fusion | flops 806354944 | bytes 8654848 | tf_op jit(solution)/shard_map/stack | solution.py:125
  84.9 9.7 %fusion.6 = f32[128,3072]{0,1:T(8,128)} fusion(bf16[1024,3072]{1,0:T(8,128)(2,1)} %param.9, bf16[128,3072]{0,1:T(8,128)(2,1)S(1)} %bitcast.68, f32[1024,128]{0,1:T(8,128)S(1)} %fusion, bf16[1024,128]{0,1:T(8,128)(2,1)S(1)} %copy.108, f32[1024]{0:T(1024)S(1)} %fusion.18), kind=kOutput, calls=%fused_computation.13 | convolution fusion | flops 1612316672 | bytes 9441280 | tf_op jit(solution)/shard_map/stack | solution.py:125
  94.6 2.2 maximum_multiply_fusion
  96.8 2.1 copy.112
  98.9 0.0 copy-start.6
  98.9 0.0 copy-start.3
  98.9 0.0 all-to-all-done
  98.9 6.7 %all-to-all-start.2 = ((f32[32,2,2,128,48]{3,4,2,1,0:T(8,128)}), f32[32,2,2,128,48]{3,4,2,1,0:T(8,128)S(1)}, u32[]{:S(2)}, u32[]{:S(2)}) async-start(f32[32,2,2,128,48]{3,4,2,1,0:T(8,128)} %copy.112), calls=%async_computation.2 | async-start | bytes 6291456 | tf_op jit(solution)/shard_map/all_to_all | solution.py:51
  105.6 0.0 sort.32.cloned.1.call-start
  105.6 0.0 copy-done.6
  105.6 1.5 iota_select_fusion
  107.1 0.6 broadcast_in_dim.44
  107.7 0.0 sort.32.cloned.1.call-update
  107.7 0.0 copy-done.3
  107.8 1.3 copy.102
  109.0 5.8 %sort.32.cloned.1.call-done = (s32[8,1024]{1,0:T(8,128)}, s32[8,1024]{1,0:T(8,128)}) async-done(((s32[8,1024]{1,0:T(8,128)}, s32[8,1024]{1,0:T(8,128)}), (s32[8,1024]{1,0:T(8,128)}, s32[8,1024]{1,0:T(8,128)})) %sort.32.cloned.1.call-update) | async-done | bytes 65552 | tf_op jit(solution)/shard_map/vmap(jit(argsort))/sort | solution.py:77
  114.8 0.7 slice.15
  115.5 8.8 %gather_fusion = f32[1024,2,48]{2,1,0:T(2,128)} fusion(f32[2,1024,48]{2,0,1:T(2,128)} %copy.102, s32[1024]{0:T(1024)S(1)} %broadcast_clamp_fusion), kind=kCustom, calls=%fused_computation | custom fusion | bytes 790528 | tf_op jit(solution)/shard_map/gather | solution.py:90
  124.3 2.1 copy.103
  126.4 48.7 %all-to-all-done.2 = f32[32,2,2,128,48]{3,4,2,1,0:T(8,128)S(1)} async-done(((f32[32,2,2,128,48]{3,4,2,1,0:T(8,128)}), f32[32,2,2,128,48]{3,4,2,1,0:T(8,128)S(1)}, u32[]{:S(2)}, u32[]{:S(2)}) %all-to-all-start.2) | async-done | bytes 3145760 | tf_op jit(solution)/shard_map/all_to_all | solution.py:51
  175.0 10.7 %all-to-all-start.1 = ((f32[2,8,128,48]{2,3,0,1:T(8,128)}), f32[2,8,128,48]{2,3,0,1:T(8,128)S(1)}, u32[]{:S(2)}, u32[]{:S(2)}) async-start(f32[2,8,128,48]{2,3,0,1:T(8,128)} %copy.103), calls=%async_computation.1 | async-start | bytes 786432 | tf_op jit(solution)/shard_map/all_to_all | solution.py:93
  185.8 0.0 sort.30.cloned.1.call-start
  185.8 0.6 broadcast_in_dim.41
  186.4 0.0 sort.30.cloned.1.call-update
  186.4 8.6 %sort.30.cloned.1.call-done = (s32[8,1024]{1,0:T(8,128)}, s32[8,1024]{1,0:T(8,128)}) async-done(((s32[8,1024]{1,0:T(8,128)}, s32[8,1024]{1,0:T(8,128)}), (s32[8,1024]{1,0:T(8,128)}, s32[8,1024]{1,0:T(8,128)})) %sort.30.cloned.1.call-update) | async-done | bytes 65552 | tf_op jit(solution)/shard_map/vmap(jit(argsort))/sort | solution.py:77
  195.0 0.7 slice.14
  195.7 0.8 reduce_sum.18
  196.5 0.6 all-to-all-done.1
  197.1 5.4 %all-to-all-start.3 = ((f32[2,2,128,48]{2,3,1,0:T(8,128)}), f32[2,2,128,48]{2,3,1,0:T(8,128)S(1)}, u32[]{:S(2)}, u32[]{:S(2)}) async-start(f32[2,2,128,48]{2,3,1,0:T(8,128)} %reduce_sum.18), calls=%async_computation.3 | async-start | bytes 196608 | tf_op jit(solution)/shard_map/all_to_all | solution.py:58
  202.5 0.0 copy-start.2
  202.5 0.0 copy-start.4
  202.5 0.0 copy-start.5
  202.5 0.6 copy.105
  203.1 0.3 broadcast_in_dim.38
  203.4 26.6 %scatter_fusion = f32[2,1024,48]{2,0,1:T(2,128)S(1)} fusion(f32[2,1024,48]{2,0,1:T(2,128)S(1)} %broadcast_in_dim.38, s32[1024]{0:T(1024)S(1)} %bitcast.72, f32[1024,2,48]{2,1,0:T(2,128)S(1)} %copy.105), kind=kCustom, calls=%fused_computation.2 | custom fusion | bytes 1183744 | tf_op jit(solution)/shard_map/scatter | solution.py:100
  230.0 0.0 all-to-all-done.3
  230.0 0.0 copy-done.2
  230.0 0.0 copy-done.4
  230.0 0.0 copy-done.5
  230.0 0.7 fusion.17
  230.7 0.1 copy.114
  230.8 4.3 %scatter_fusion.1 = f32[2,1024,48]{2,0,1:T(2,128)S(1)} fusion(f32[2,1024,48]{2,0,1:T(2,128)S(1)} %scatter_fusion, s32[128]{0:T(128)S(1)} %compare_select_fusion.2, f32[128,2,48]{2,1,0:T(2,128)S(1)} %copy.114), kind=kCustom, calls=%fused_computation.3 | custom fusion | bytes 147968 | tf_op jit(solution)/shard_map/scatter | solution.py:132
  235.1 1.1 copy.115
  (10 shorter events, 0.1 us)
Async XLA Ops:
  8.0 67.6 %all-gather.3.cloned.1.call-start = ((), (), s32[]{:S(2)}) async-start(), calls=%async_computation.4 | async-start | bytes 1769472 | tf_op jit(solution)/shard_map/all_gather | solution.py:33
  11.0 64.7 %copy-start.1 = (f32[128,2,48]{0,2,1:T(8,128)}, f32[128,2,48]{0,2,1:T(8,128)S(1)}, u32[]{:S(2)}) copy-start(f32[128,2,48]{0,2,1:T(8,128)S(1)} %copy.107) | copy-start | bytes 147460
  34.5 64.4 %all-to-all-start = ((s32[8,1,1024]{2,1,0:T(1,128)}), s32[8,1,1024]{2,1,0:T(1,128)}, u32[]{:S(2)}, u32[]{:S(2)}) async-start(s32[8,1,1024]{2,1,0:T(1,128)} %broadcast_in_dim.42), calls=%async_computation | async-start | bytes 65536 | tf_op jit(solution)/shard_map/all_to_all | solution.py:23
  75.6 3.3 %copy-start = (bf16[1024,3072]{1,0:T(8,128)(2,1)S(1)}, bf16[1024,3072]{1,0:T(8,128)(2,1)}, u32[]{:S(2)}) copy-start(bf16[1024,3072]{1,0:T(8,128)(2,1)} %param.9) | copy-start | bytes 18874372
  98.9 6.8 %copy-start.6 = (s32[1024]{0:T(1024)S(1)}, s32[1024]{0:T(1024)}, u32[]{:S(2)}) copy-start(s32[1024]{0:T(1024)} %param.17) | copy-start | bytes 12292
  98.9 8.9 %copy-start.3 = (f32[2,1024,48]{1,2,0:T(8,128)S(1)}, f32[2,1024,48]{1,2,0:T(8,128)}, u32[]{:S(2)}) copy-start(f32[2,1024,48]{1,2,0:T(8,128)} %param.16) | copy-start | bytes 1179652
  98.9 76.2 %all-to-all-start.2 = ((f32[32,2,2,128,48]{3,4,2,1,0:T(8,128)}), f32[32,2,2,128,48]{3,4,2,1,0:T(8,128)S(1)}, u32[]{:S(2)}, u32[]{:S(2)}) async-start(f32[32,2,2,128,48]{3,4,2,1,0:T(8,128)} %copy.112), calls=%async_computation.2 | async-start | bytes 6291456 | tf_op jit(solution)/shard_map/all_to_all | solution.py:51
  105.6 9.3 %sort.32.cloned.1.call-start = ((), (), s32[]{:S(2)}) async-start(), calls=%async_computation.6 | async-start | bytes 196640 | tf_op jit(solution)/shard_map/vmap(jit(argsort))/sort | solution.py:77
  175.0 22.1 %all-to-all-start.1 = ((f32[2,8,128,48]{2,3,0,1:T(8,128)}), f32[2,8,128,48]{2,3,0,1:T(8,128)S(1)}, u32[]{:S(2)}, u32[]{:S(2)}) async-start(f32[2,8,128,48]{2,3,0,1:T(8,128)} %copy.103), calls=%async_computation.1 | async-start | bytes 786432 | tf_op jit(solution)/shard_map/all_to_all | solution.py:93
  185.8 9.3 %sort.30.cloned.1.call-start = ((), (), s32[]{:S(2)}) async-start(), calls=%async_computation.5 | async-start | bytes 196640 | tf_op jit(solution)/shard_map/vmap(jit(argsort))/sort | solution.py:77
  197.1 32.9 %all-to-all-start.3 = ((f32[2,2,128,48]{2,3,1,0:T(8,128)}), f32[2,2,128,48]{2,3,1,0:T(8,128)S(1)}, u32[]{:S(2)}, u32[]{:S(2)}) async-start(f32[2,2,128,48]{2,3,1,0:T(8,128)} %reduce_sum.18), calls=%async_computation.3 | async-start | bytes 196608 | tf_op jit(solution)/shard_map/all_to_all | solution.py:58
  202.5 27.5 %copy-start.2 = (f32[128,2,48]{0,2,1:T(8,128)S(1)}, f32[128,2,48]{0,2,1:T(8,128)}, u32[]{:S(2)}) copy-start(f32[128,2,48]{0,2,1:T(8,128)} %copy-done.1) | copy-start | bytes 147460
  202.5 27.5 %copy-start.4 = (f32[2,128,48]{1,2,0:T(8,128)S(1)}, f32[2,128,48]{1,2,0:T(8,128)}, u32[]{:S(2)}) copy-start(f32[2,128,48]{1,2,0:T(8,128)} %param.13) | copy-start | bytes 147460
  202.5 27.5 %copy-start.5 = (f32[2,128,48]{1,2,0:T(8,128)S(1)}, f32[2,128,48]{1,2,0:T(8,128)}, u32[]{:S(2)}) copy-start(f32[2,128,48]{1,2,0:T(8,128)} %param.14) | copy-start | bytes 147460
Sparse Core Ops, SparseCore 0:
  33.3 42.2 all-gather.2
Sparse Core Ops, SparseCore 1:
  109.1 5.4 sort.36.cloned.1.call-done
  189.3 5.4 sort.34.cloned.1.call-done
  (2 shorter events, 0.0 us)
where the time goes:
time: 245 us; the launch traced here: 244 us
  waiting for transfers between devices  78.9 us (32%)
  local copies, waits for them, and re-layouts  72.2 us (29%)
  starting transfers between devices  32.6 us (13%)
  blocking collectives  22.2 us (9%)
  between operations  16.3 us (7%)
  matrix products  15.7 us (6%)
  other arithmetic  5.79 us (2%)
    all_to_all x1, waiting for transfers between devices, sum_at_owner(): lax.all_to_all(tiles, axis, split_axis=0, concat_axis=0, tiled=True)  48.7 us
    all_gather x1, waiting for transfers between devices, stacked_from(): tiles = lax.all_gather(tiles, axes[k], axis=0, tiled=True)  29.6 us
    scatter x1, local copies, waits for them, and re-layouts, return_cold(): received = jnp.zeros_like(cold_blocks).at[:, take_rows.reshape(-1), :].se...  26.6 us
    all_gather x2, blocking collectives, stacked_from(): tiles = lax.all_gather(tiles, axes[k], axis=0, tiled=True)  22.2 us
    sort x4, local copies, waits for them, and re-layouts, rows_with(): return jnp.argsort(sort_key, stable=True)[:capacity]  14.5 us
    another operation x2, matrix products, per_device(): jnp.stack([contract_first(d_gate, tokens), contract_first(d_up, tokens)])  13.5 us
    all_to_all x1, starting transfers between devices, return_cold(): lax.all_to_all(packed, 'expert', split_axis=1, concat_axis=1, tiled=True)  10.7 us
    all_to_all x1, starting transfers between devices, sent_to_all(): return lax.all_to_all(copies, axis, split_axis=0, concat_axis=0, tiled=True)  9.76 us
  transfers between devices with their start and end apart: 5, of which 3 were waited for; matrix products, arithmetic and copies ran while one was open for 28% of the time, Pallas kernels for 0%

commit v1 on v0

--- a/solution.py
+++ b/solution.py
@@ -30,7 +30,9 @@
 def stacked_from(value, axes, order):
     tiles = value[None]
     for k in order:
-        tiles = lax.all_gather(tiles, axes[k], axis=0, tiled=True)
+        tiles = jnp.concatenate(
+            lax.all_to_all(jnp.stack([tiles] * lax.axis_size(axes[k])), axes[k], 0, 0), axis=0
+        )
     block = [lax.axis_size(axes[k]) for k in reversed(order)]
     tiles = tiles.reshape(*block, *value.shape)
     turned = sorted(range(len(order)), key=lambda place: order[len(order) - 1 - place])

time: 245 us -> 254 us (1.037)
  waiting for transfers between devices: 78.9 us -> 88.4 us
  blocking collectives: 22.2 us -> 26.6 us
  starting transfers between devices: 32.6 us -> 29.6 us
    all_to_all x0 -> x1, waiting for transfers between devices: none -> 36.9 us  [stacked_from(): lax.all_to_all(jnp.stack([tiles] * lax.axis_size(axes[k])), axes[k], 0, 0)]
    all_gather x1 -> x0, waiting for transfers between devices: 29.6 us -> none  [stacked_from(): tiles = lax.all_gather(tiles, axes[k], axis=0, tiled=True)]
    all_to_all x0 -> x2, blocking collectives: none -> 26.6 us  [stacked_from(): lax.all_to_all(jnp.stack([tiles] * lax.axis_size(axes[k])), axes[k], 0, 0)]
    all_gather x2 -> x0, blocking collectives: 22.2 us -> none  [stacked_from(): tiles = lax.all_gather(tiles, axes[k], axis=0, tiled=True)]
    all_to_all x0 -> x1, starting transfers between devices: none -> 6.82 us  [stacked_from(): lax.all_to_all(jnp.stack([tiles] * lax.axis_size(axes[k])), axes[k], 0, 0)]
    all_to_all x1, starting transfers between devices: 10.7 us -> 7.8 us  [return_cold(): lax.all_to_all(packed, 'expert', split_axis=1, concat_axis=1, tiled=True)]
    all_to_all x1, waiting for transfers between devices: 48.7 us -> 51.3 us  [sum_at_owner(): lax.all_to_all(tiles, axis, split_axis=0, concat_axis=0, tiled=True)]
    unnamed x20 -> x22, local copies, waits for them, and re-layouts: 6.4 us -> 6.65 us
  transfers between devices with their start and end apart: 5 -> 5, of which waited for: 3 -> 3; matrix products, arithmetic and copies ran while one was open for 28% -> 26% of each run, Pallas kernels for 0% -> 0%
where the time goes in v1:
time: 254 us; the launch traced here: 253 us
  waiting for transfers between devices  88.4 us (35%)
  local copies, waits for them, and re-layouts  72.3 us (28%)
  starting transfers between devices  29.6 us (12%)
  blocking collectives  26.6 us (10%)
  matrix products  15.7 us (6%)
  between operations  14.9 us (6%)
  other arithmetic  5.8 us (2%)
    all_to_all x1, waiting for transfers between devices, sum_at_owner(): lax.all_to_all(tiles, axis, split_axis=0, concat_axis=0, tiled=True)  51.3 us
    all_to_all x1, waiting for transfers between devices, stacked_from(): lax.all_to_all(jnp.stack([tiles] * lax.axis_size(axes[k])), axes[k], 0, 0)  36.9 us
    all_to_all x2, blocking collectives, stacked_from(): lax.all_to_all(jnp.stack([tiles] * lax.axis_size(axes[k])), axes[k], 0, 0)  26.6 us
    scatter x1, local copies, waits for them, and re-layouts, return_cold(): received = jnp.zeros_like(cold_blocks).at[:, take_rows.reshape(-1), :].se...  26.6 us
    sort x4, local copies, waits for them, and re-layouts, rows_with(): return jnp.argsort(sort_key, stable=True)[:capacity]  15.1 us
    another operation x2, matrix products, per_device(): jnp.stack([contract_first(d_gate, tokens), contract_first(d_up, tokens)])  13.5 us
    gather x1, local copies, waits for them, and re-layouts, return_cold(): cold_blocks[:, send_rows.reshape(-1), :]  8.77 us
    all_to_all x1, starting transfers between devices, return_cold(): lax.all_to_all(packed, 'expert', split_axis=1, concat_axis=1, tiled=True)  7.8 us
  transfers between devices with their start and end apart: 5, of which 3 were waited for; matrix products, arithmetic and copies ran while one was open for 26% of the time, Pallas kernels for 0%

profile of v1, /device:TPU:1, one launch (start us, length us, event | category | flops | bytes accessed | tf_op | source)
XLA Modules:
  0.0 253.5 jit_solution(6226526137532996484)
XLA Ops:
  7.2 0.7 compare_select_fusion.2
  7.8 1.4 copy.111
  9.3 0.0 copy-start.4
  9.3 0.7 gather_fusion.1
  10.0 0.1 copy.112
  10.1 0.0 copy-start.1
  10.1 0.0 copy-start.7
  10.2 17.6 %all_to_all.39 = bf16[2,1,2,128,48]{3,4,2,1,0:T(8,128)(2,1)S(1)} all-to-all(bf16[2,1,2,128,48]{3,4,2,1,0:T(8,128)(2,1)S(1)} %pad_maximum_fusion), channel_id=1, replica_groups=mesh['dp_0'=2,'dp_1'=4,'dp_2'=8,'expert'=8] {'dp_0'}, dimensions={0} | all-to-all | bytes 98304 | tf_op jit(solution)/shard_map/all_to_all | solution.py:34
  27.8 0.0 copy-done.1
  27.8 9.0 %all_to_all.40 = bf16[4,2,2,128,48]{3,4,2,1,0:T(8,128)(2,1)S(1)} all-to-all(bf16[4,2,2,128,48]{3,4,2,1,0:T(8,128)(2,1)S(1)} %stack.19), channel_id=1, replica_groups=mesh['dp_0'=2,'dp_1'=4,'dp_2'=8,'expert'=8] {'dp_1'}, dimensions={0} | all-to-all | bytes 393216 | tf_op jit(solution)/shard_map/all_to_all | solution.py:34
  36.8 1.4 stack.20
  38.2 6.8 %all-to-all-start.4 = ((bf16[8,8,2,128,48]{3,4,2,1,0:T(8,128)(2,1)}), bf16[8,8,2,128,48]{3,4,2,1,0:T(8,128)(2,1)S(1)}, u32[]{:S(2)}, u32[]{:S(2)}) async-start(bf16[8,8,2,128,48]{3,4,2,1,0:T(8,128)(2,1)} %stack.20), calls=%async_computation.4 | async-start | bytes 3145728 | tf_op jit(solution)/shard_map/all_to_all | solution.py:34
  45.1 0.0 copy-done.4
  45.1 0.1 copy.113
  45.9 36.9 %all-to-all-done.4 = bf16[8,8,2,128,48]{3,4,2,1,0:T(8,128)(2,1)S(1)} async-done(((bf16[8,8,2,128,48]{3,4,2,1,0:T(8,128)(2,1)}), bf16[8,8,2,128,48]{3,4,2,1,0:T(8,128)(2,1)S(1)}, u32[]{:S(2)}, u32[]{:S(2)}) %all-to-all-start.4) | async-done | bytes 1572896 | tf_op jit(solution)/shard_map/all_to_all | solution.py:34
  82.8 0.0 copy-done.7
  82.8 0.6 broadcast_in_dim.41
  83.5 7.5 %all-to-all-start = ((s32[8,1,1024]{2,1,0:T(1,128)}), s32[8,1,1024]{2,1,0:T(1,128)}, u32[]{:S(2)}, u32[]{:S(2)}) async-start(s32[8,1,1024]{2,1,0:T(1,128)} %broadcast_in_dim.41), calls=%async_computation | async-start | bytes 65536 | tf_op jit(solution)/shard_map/all_to_all | solution.py:23
  91.0 0.0 copy-start
  91.0 0.1 copy.114
  91.1 0.1 fusion.26
  91.2 2.5 copy-done
  93.7 2.2 fusion
  95.9 3.8 %fusion.10 = f32[128,3072]{0,1:T(8,128)} fusion(bf16[1024,3072]{1,0:T(8,128)(2,1)S(1)} %copy-done, f32[1024,128]{0,1:T(8,128)S(1)} %fusion, bf16[1024,128]{0,1:T(8,128)(2,1)S(1)} %copy.113, f32[1024]{0:T(1024)S(1)} %fusion.19), kind=kOutput, calls=%fused_computation.21 | convolution fusion | flops 806354944 | bytes 8654848 | tf_op jit(solution)/shard_map/stack | solution.py:127
  99.8 9.7 %fusion.6 = f32[128,3072]{0,1:T(8,128)} fusion(bf16[1024,3072]{1,0:T(8,128)(2,1)} %param.9, bf16[128,3072]{0,1:T(8,128)(2,1)S(1)} %bitcast.74, f32[1024,128]{0,1:T(8,128)S(1)} %fusion, bf16[1024,128]{0,1:T(8,128)(2,1)S(1)} %copy.113, f32[1024]{0:T(1024)S(1)} %fusion.19), kind=kOutput, calls=%fused_computation.13 | convolution fusion | flops 1612316672 | bytes 9441280 | tf_op jit(solution)/shard_map/stack | solution.py:127
  109.4 2.2 maximum_multiply_fusion
  111.6 2.1 copy.117
  113.7 0.0 copy-start.3
  113.7 0.0 all-to-all-done
  113.7 4.2 %all-to-all-start.5 = ((f32[32,2,2,128,48]{3,4,2,1,0:T(8,128)}), f32[32,2,2,128,48]{3,4,2,1,0:T(8,128)S(1)}, u32[]{:S(2)}, u32[]{:S(2)}) async-start(f32[32,2,2,128,48]{3,4,2,1,0:T(8,128)} %copy.117), calls=%async_computation.5 | async-start | bytes 6291456 | tf_op jit(solution)/shard_map/all_to_all | solution.py:53
  117.9 0.0 sort.32.cloned.1.call-start
  118.0 1.5 iota_select_fusion
  119.4 0.6 broadcast_in_dim.43
  120.0 0.0 sort.32.cloned.1.call-update
  120.1 0.0 copy-done.3
  120.1 1.3 copy.107
  121.3 6.2 %sort.32.cloned.1.call-done = (s32[8,1024]{1,0:T(8,128)}, s32[8,1024]{1,0:T(8,128)}) async-done(((s32[8,1024]{1,0:T(8,128)}, s32[8,1024]{1,0:T(8,128)}), (s32[8,1024]{1,0:T(8,128)}, s32[8,1024]{1,0:T(8,128)})) %sort.32.cloned.1.call-update) | async-done | bytes 65552 | tf_op jit(solution)/shard_map/vmap(jit(argsort))/sort | solution.py:79
  127.5 0.7 slice.15
  128.2 8.8 %gather_fusion = f32[1024,2,48]{2,1,0:T(2,128)} fusion(f32[2,1024,48]{2,0,1:T(2,128)} %copy.107, s32[1024]{0:T(1024)S(1)} %broadcast_clamp_fusion), kind=kCustom, calls=%fused_computation | custom fusion | bytes 790528 | tf_op jit(solution)/shard_map/gather | solution.py:92
  137.0 2.1 copy.108
  139.1 51.3 %all-to-all-done.5 = f32[32,2,2,128,48]{3,4,2,1,0:T(8,128)S(1)} async-done(((f32[32,2,2,128,48]{3,4,2,1,0:T(8,128)}), f32[32,2,2,128,48]{3,4,2,1,0:T(8,128)S(1)}, u32[]{:S(2)}, u32[]{:S(2)}) %all-to-all-start.5) | async-done | bytes 3145760 | tf_op jit(solution)/shard_map/all_to_all | solution.py:53
  190.4 7.8 %all-to-all-start.1 = ((f32[2,8,128,48]{2,3,0,1:T(8,128)}), f32[2,8,128,48]{2,3,0,1:T(8,128)S(1)}, u32[]{:S(2)}, u32[]{:S(2)}) async-start(f32[2,8,128,48]{2,3,0,1:T(8,128)} %copy.108), calls=%async_computation.1 | async-start | bytes 786432 | tf_op jit(solution)/shard_map/all_to_all | solution.py:95
  198.2 0.0 sort.30.cloned.1.call-start
  198.2 0.6 broadcast_in_dim.40
  198.8 0.1 sort.30.cloned.1.call-update
  198.9 8.9 %sort.30.cloned.1.call-done = (s32[8,1024]{1,0:T(8,128)}, s32[8,1024]{1,0:T(8,128)}) async-done(((s32[8,1024]{1,0:T(8,128)}, s32[8,1024]{1,0:T(8,128)}), (s32[8,1024]{1,0:T(8,128)}, s32[8,1024]{1,0:T(8,128)})) %sort.30.cloned.1.call-update) | async-done | bytes 65552 | tf_op jit(solution)/shard_map/vmap(jit(argsort))/sort | solution.py:79
  207.8 0.7 slice.14
  208.5 0.8 reduce_sum.18
  209.3 0.2 all-to-all-done.1
  209.5 3.3 %all-to-all-start.6 = ((f32[2,2,128,48]{2,3,1,0:T(8,128)}), f32[2,2,128,48]{2,3,1,0:T(8,128)S(1)}, u32[]{:S(2)}, u32[]{:S(2)}) async-start(f32[2,2,128,48]{2,3,1,0:T(8,128)} %reduce_sum.18), calls=%async_computation.6 | async-start | bytes 196608 | tf_op jit(solution)/shard_map/all_to_all | solution.py:60
  212.8 0.0 copy-start.2
  212.8 0.0 copy-start.5
  212.8 0.0 copy-start.6
  212.9 0.6 copy.110
  213.4 0.3 broadcast_in_dim.37
  213.7 26.6 %scatter_fusion = f32[2,1024,48]{2,0,1:T(2,128)S(1)} fusion(f32[2,1024,48]{2,0,1:T(2,128)S(1)} %broadcast_in_dim.37, s32[1024]{0:T(1024)S(1)} %bitcast.78, f32[1024,2,48]{2,1,0:T(2,128)S(1)} %copy.110), kind=kCustom, calls=%fused_computation.2 | custom fusion | bytes 1183744 | tf_op jit(solution)/shard_map/scatter | solution.py:102
  240.3 0.0 all-to-all-done.6
  240.4 0.0 copy-done.2
  240.4 0.0 copy-done.5
  240.4 0.0 copy-done.6
  240.4 0.7 fusion.17
  241.0 0.1 copy.119
  241.2 4.3 %scatter_fusion.1 = f32[2,1024,48]{2,0,1:T(2,128)S(1)} fusion(f32[2,1024,48]{2,0,1:T(2,128)S(1)} %scatter_fusion, s32[128]{0:T(128)S(1)} %compare_select_fusion.2, f32[128,2,48]{2,1,0:T(2,128)S(1)} %copy.119), kind=kCustom, calls=%fused_computation.3 | custom fusion | bytes 147968 | tf_op jit(solution)/shard_map/scatter | solution.py:134
  245.5 1.1 copy.120
  (12 shorter events, 0.1 us)
Async XLA Ops:
  9.3 35.8 %copy-start.4 = (bf16[1024,128]{1,0:T(8,128)(2,1)S(1)}, bf16[1024,128]{1,0:T(8,128)(2,1)}, u32[]{:S(2)}) copy-start(bf16[1024,128]{1,0:T(8,128)(2,1)} %param.10) | copy-start | bytes 786436
  10.1 17.7 %copy-start.1 = (f32[128,2,48]{0,2,1:T(8,128)}, f32[128,2,48]{0,2,1:T(8,128)S(1)}, u32[]{:S(2)}) copy-start(f32[128,2,48]{0,2,1:T(8,128)S(1)} %copy.112) | copy-start | bytes 147460
  10.1 72.7 %copy-start.7 = (s32[1024]{0:T(1024)S(1)}, s32[1024]{0:T(1024)}, u32[]{:S(2)}) copy-start(s32[1024]{0:T(1024)} %param.17) | copy-start | bytes 12292
  38.2 44.6 %all-to-all-start.4 = ((bf16[8,8,2,128,48]{3,4,2,1,0:T(8,128)(2,1)}), bf16[8,8,2,128,48]{3,4,2,1,0:T(8,128)(2,1)S(1)}, u32[]{:S(2)}, u32[]{:S(2)}) async-start(bf16[8,8,2,128,48]{3,4,2,1,0:T(8,128)(2,1)} %stack.20), calls=%async_computation.4 | async-start | bytes 3145728 | tf_op jit(solution)/shard_map/all_to_all | solution.py:34
  83.5 30.2 %all-to-all-start = ((s32[8,1,1024]{2,1,0:T(1,128)}), s32[8,1,1024]{2,1,0:T(1,128)}, u32[]{:S(2)}, u32[]{:S(2)}) async-start(s32[8,1,1024]{2,1,0:T(1,128)} %broadcast_in_dim.41), calls=%async_computation | async-start | bytes 65536 | tf_op jit(solution)/shard_map/all_to_all | solution.py:23
  91.0 2.8 %copy-start = (bf16[1024,3072]{1,0:T(8,128)(2,1)S(1)}, bf16[1024,3072]{1,0:T(8,128)(2,1)}, u32[]{:S(2)}) copy-start(bf16[1024,3072]{1,0:T(8,128)(2,1)} %param.9) | copy-start | bytes 18874372
  113.7 6.4 %copy-start.3 = (f32[2,1024,48]{1,2,0:T(8,128)S(1)}, f32[2,1024,48]{1,2,0:T(8,128)}, u32[]{:S(2)}) copy-start(f32[2,1024,48]{1,2,0:T(8,128)} %param.16) | copy-start | bytes 1179652
  113.7 76.7 %all-to-all-start.5 = ((f32[32,2,2,128,48]{3,4,2,1,0:T(8,128)}), f32[32,2,2,128,48]{3,4,2,1,0:T(8,128)S(1)}, u32[]{:S(2)}, u32[]{:S(2)}) async-start(f32[32,2,2,128,48]{3,4,2,1,0:T(8,128)} %copy.117), calls=%async_computation.5 | async-start | bytes 6291456 | tf_op jit(solution)/shard_map/all_to_all | solution.py:53
  117.9 9.7 %sort.32.cloned.1.call-start = ((), (), s32[]{:S(2)}) async-start(), calls=%async_computation.8 | async-start | bytes 196640 | tf_op jit(solution)/shard_map/vmap(jit(argsort))/sort | solution.py:79
  190.4 19.1 %all-to-all-start.1 = ((f32[2,8,128,48]{2,3,0,1:T(8,128)}), f32[2,8,128,48]{2,3,0,1:T(8,128)S(1)}, u32[]{:S(2)}, u32[]{:S(2)}) async-start(f32[2,8,128,48]{2,3,0,1:T(8,128)} %copy.108), calls=%async_computation.1 | async-start | bytes 786432 | tf_op jit(solution)/shard_map/all_to_all | solution.py:95
  198.2 9.6 %sort.30.cloned.1.call-start = ((), (), s32[]{:S(2)}) async-start(), calls=%async_computation.7 | async-start | bytes 196640 | tf_op jit(solution)/shard_map/vmap(jit(argsort))/sort | solution.py:79
  209.5 30.9 %all-to-all-start.6 = ((f32[2,2,128,48]{2,3,1,0:T(8,128)}), f32[2,2,128,48]{2,3,1,0:T(8,128)S(1)}, u32[]{:S(2)}, u32[]{:S(2)}) async-start(f32[2,2,128,48]{2,3,1,0:T(8,128)} %reduce_sum.18), calls=%async_computation.6 | async-start | bytes 196608 | tf_op jit(solution)/shard_map/all_to_all | solution.py:60
  212.8 27.5 %copy-start.2 = (f32[128,2,48]{0,2,1:T(8,128)S(1)}, f32[128,2,48]{0,2,1:T(8,128)}, u32[]{:S(2)}) copy-start(f32[128,2,48]{0,2,1:T(8,128)} %copy-done.1) | copy-start | bytes 147460
  212.8 27.5 %copy-start.5 = (f32[2,128,48]{1,2,0:T(8,128)S(1)}, f32[2,128,48]{1,2,0:T(8,128)}, u32[]{:S(2)}) copy-start(f32[2,128,48]{1,2,0:T(8,128)} %param.13) | copy-start | bytes 147460
  212.8 27.5 %copy-start.6 = (f32[2,128,48]{1,2,0:T(8,128)S(1)}, f32[2,128,48]{1,2,0:T(8,128)}, u32[]{:S(2)}) copy-start(f32[2,128,48]{1,2,0:T(8,128)} %param.14) | copy-start | bytes 147460
Sparse Core Ops, SparseCore 0:
  121.7 5.5 sort.36.cloned.1.call-done
  202.0 5.4 sort.34.cloned.1.call-done
  (2 shorter events, 0.0 us)
